TPU v7x, 256 devices: a whole 4x4x8 slice. The times are simulated.
256 devices in a mesh: occ: 64 (over z, y, core), ao: 4 (over x).
Axes of the slice: x: 4, y: 4, z: 8, core: 2. Of those that a mesh axis runs over, the one named last changes fastest.
Arguments:
- amplitudes: bfloat16 [8, 5120, 19456], P(None, 'occ', 'ao'), may hold values from -6 to 6
- occ_coef: bfloat16 [512, 5120], P(None, 'occ'), may hold values from -0.25 to 0.25
- vir_coef: bfloat16 [512, 19456], P('occ', 'ao'), may hold values from -0.25 to 0.25
- occ_energy: float32 [5120], P('occ'), may hold values from -1.5 to -0.3
- vir_energy: float32 [19456], P('ao'), may hold values from 0.05 to 2.5
- kernel: float32 [512], replicated, may hold values from 2 to 10
Outputs:
- residual: bfloat16 [8, 5120, 19456], P(None, 'occ', 'ao')
- projected: float32 [8, 8], replicated
All inputs are finite; a program needn't handle non-finite values.
Results may differ from a plain program's by a relative error of at most 0.0049.
Values may be sent and summed in bfloat16 or wider, within the bound.
A program may use at most 128 MiB of HBM per device.

v0:
```python
import jax
import jax.numpy as jnp
from jax import lax
from jax.sharding import Mesh
from jax.sharding import PartitionSpec as P

OCC = ("occ_0", "occ_1", "occ_2")


def laid_out(tiles, dim):
    tiles = jnp.moveaxis(tiles, 0, dim)
    dims = tiles.shape
    return tiles.reshape(*dims[:dim], dims[dim] * dims[dim + 1], *dims[dim + 2 :])


def stacked_from(x, axes, order):
    tiles = x
    for k in order:
        tiles = lax.all_gather(tiles, axes[k])
    done = order[::-1]
    back = [done.index(k) for k in range(len(axes))]
    tiles = tiles.transpose(*back, *range(len(axes), tiles.ndim))
    return tiles.reshape(-1, *x.shape)


def gather_axes(x, axes, order, dim):
    return laid_out(stacked_from(x, axes, order), dim)


def sent_to_all(x, axis):
    copies = jnp.broadcast_to(x, (lax.axis_size(axis), *x.shape))
    return lax.all_to_all(copies, axis, split_axis=0, concat_axis=0, tiled=True)


def over_copies(x, axis):
    everything = sent_to_all(x, axis)
    return jnp.sum(everything, axis=0)


def one_axis_at_a_time(x, axes):
    far, near = axes
    return over_copies(over_copies(x, near), far)


def packed_total(arrays, axis):
    vector, at, finished = (jnp.concatenate([a.reshape(-1) for a in arrays]), 0, [])
    running = one_axis_at_a_time(vector, axis)
    for a in arrays:
        finished.append(running[at : at + a.size].reshape(a.shape))
        at += a.size
    return tuple(finished)


def shards(amplitudes, occ_coef, vir_coef, occ_energy, vir_energy, kernel):
    trials, occ_dev, vir_dev = amplitudes.shape
    row_total = occ_coef.shape[0]
    flat_amps = amplitudes.reshape(trials * occ_dev, vir_dev)
    occ_trans = occ_coef.T.astype(jnp.float32)
    whole_rows = gather_axes(vir_coef, OCC, (1, 0, 2), 0)
    row_count = whole_rows.shape[0]
    half_done = lax.dot_general(
        flat_amps, whole_rows, (((1,), (1,)), ((), ())), preferred_element_type=jnp.float32
    )
    half_done = half_done.reshape(trials, occ_dev, row_count)
    partial_value = jnp.sum(half_done * occ_trans[None], axis=1)
    amps_rows = amplitudes.reshape(trials, occ_dev * vir_dev)
    correlation_local = jnp.dot(amps_rows, amps_rows.T, preferred_element_type=jnp.float32)
    density, correlation = packed_total(
        (partial_value, correlation_local), ("occ_0", ("occ_1", "occ_2", "ao"))
    )
    potential = kernel[None, :] * density
    weighted = (
        (occ_trans[None] * potential[:, None, :])
        .astype(jnp.bfloat16)
        .reshape(trials * occ_dev, row_total)
    )
    coupling = jnp.dot(weighted, whole_rows, preferred_element_type=jnp.float32)
    energy_gaps = vir_energy[None, :] - occ_energy[:, None]
    sigma_block = energy_gaps[None] * amplitudes.astype(jnp.float32) + coupling.reshape(
        trials, occ_dev, vir_dev
    )

    def gram_column(sigma_one):
        return jnp.sum(amplitudes.astype(jnp.float32) * sigma_one[None], axis=(1, 2))

    gram_local = lax.map(gram_column, sigma_block).T
    gram = one_axis_at_a_time(gram_local, (("occ_0", "occ_1"), ("occ_2", "ao")))
    norms = jnp.diagonal(correlation) + 1e-06
    ritz_values = jnp.diagonal(gram) / norms
    residual = (sigma_block - ritz_values[:, None, None] * amplitudes.astype(jnp.float32)).astype(
        jnp.bfloat16
    )
    projected = gram / jnp.sqrt(norms[:, None] * norms[None, :])
    return (residual, projected)


def solution(mesh):
    torus = Mesh(mesh.devices.reshape(8, 4, 2, mesh.shape["ao"]), ("occ_0", "occ_1", "occ_2", "ao"))
    in_specs = (P(None, OCC, "ao"), P(None, OCC), P(OCC, "ao"), P(OCC), P("ao"), P())
    out_specs = (P(None, OCC, "ao"), P())
    return jax.shard_map(
        shards, mesh=torus, in_specs=in_specs, out_specs=out_specs, check_vma=False
    )
```

profile of v0, /device:TPU:1, one launch (start us, length us, event | category | flops | bytes accessed | tf_op | source)
XLA Modules:
  0.0 227.8 jit_solution(628546609055279525)
XLA Ops:
  7.2 0.0 all-gather.6.cloned.1.call-start
  7.2 12.8 %all-gather = bf16[32,4864]{1,0:T(8,128)(2,1)} all-gather(bf16[8,4864]{1,0:T(8,128)(2,1)} %param.10), channel_id=2, replica_groups=mesh['occ_0'=8,'occ_1'=4,'occ_2'=2,'ao'=4] {'occ_1'}, dimensions={0}, use_global_device_ids=true | all-gather | bytes 389120 | tf_op jit(solution)/shard_map/all_gather | solution.py:19
  20.0 0.0 all-gather.6.cloned.1.call-update
  20.1 0.0 all-gather.8.cloned.1.call-start
  20.1 42.1 %all-gather.6.cloned.1.call-done = bf16[32,8,4864]{2,1,0:T(8,128)(2,1)} async-done(((bf16[4,8,4864]{2,1,0:T(8,128)(2,1)}), bf16[32,8,4864]{2,1,0:T(8,128)(2,1)}) %all-gather.6.cloned.1.call-update) | async-done | bytes 2490384 | tf_op jit(solution)/shard_map/all_gather | solution.py:19
  62.2 0.0 all-gather.8.cloned.1.call-update
  62.3 11.2 %fusion.6 = f32[8,8]{1,0:T(8,128)S(1)} fusion(bf16[8,80,4864]{2,1,0:T(8,128)(2,1)} %param.8), kind=kOutput, calls=%fused_computation.14 | convolution fusion | flops 49807360 | bytes 6226176 | tf_op jit(solution)/shard_map/dot_general | solution.py:67
  73.5 0.1 reshape.99
  73.6 13.5 %all-gather.8.cloned.1.call-done = bf16[16,4,8,4864]{3,2,1,0:T(8,128)(2,1)} async-done(((bf16[8,4,8,4864]{3,2,1,0:T(8,128)(2,1)}), bf16[16,4,8,4864]{3,2,1,0:T(8,128)(2,1)}) %all-gather.8.cloned.1.call-update) | async-done | bytes 4980752 | tf_op jit(solution)/shard_map/all_gather | solution.py:19
  87.1 2.9 %copy.27 = bf16[8,4,2,8,4864]{4,3,2,1,0:T(8,128)(2,1)S(1)} copy(bf16[8,4,2,8,4864]{4,3,1,0,2:T(8,128)(2,1)} %bitcast.31) | data formatting | bytes 9961472 | tf_op jit(solution)/shard_map/transpose | solution.py:22
  90.0 0.7 slice-done.1
  90.8 3.4 %fusion.5 = f32[8,512]{1,0:T(8,128)S(1)} fusion(bf16[8,80,4864]{2,1,0:T(8,128)(2,1)S(1)} %bitcast.28, bf16[512,4864,1]{1,0,2:T(8,128)(2,1)S(1)} %bitcast.29, f32[80,512]{1,0:T(8,128)S(1)} %convert_bitcast_fusion), kind=kOutput, calls=%fused_computation.13 | convolution fusion | flops 3188322304 | bytes 11386880 | tf_op jit(solution)/shard_map/dot_general | solution.py:61
  94.2 0.3 broadcast_in_dim.21
  94.5 18.2 %all_to_all.22 = f32[32,1,4160]{2,1,0:T(1,128)S(1)} all-to-all(f32[32,1,4160]{2,1,0:T(1,128)S(1)} %broadcast_in_dim.21), channel_id=1, replica_groups=mesh['occ_0'=8,'occ_1'=4,'occ_2'=2,'ao'=4] {'occ_1','occ_2','ao'}, dimensions={0} | all-to-all | bytes 1064960 | tf_op jit(solution)/shard_map/all_to_all | solution.py:32
  112.7 0.3 reduce_sum.55
  113.0 0.7 broadcast_in_dim.22
  113.7 6.7 %all-to-all-start.1 = ((f32[8,1,4160]{2,1,0:T(1,128)}), f32[8,1,4160]{2,1,0:T(1,128)S(1)}, u32[]{:S(2)}, u32[]{:S(2)}) async-start(f32[8,1,4160]{2,1,0:T(1,128)} %broadcast_in_dim.22), calls=%async_computation.1 | async-start | bytes 270336 | tf_op jit(solution)/shard_map/all_to_all | solution.py:32
  120.5 0.2 broadcast_subtract_fusion
  120.7 7.7 %all-to-all-done.1 = f32[8,1,4160]{2,1,0:T(1,128)S(1)} async-done(((f32[8,1,4160]{2,1,0:T(1,128)}), f32[8,1,4160]{2,1,0:T(1,128)S(1)}, u32[]{:S(2)}, u32[]{:S(2)}) %all-to-all-start.1) | async-done | bytes 133152 | tf_op jit(solution)/shard_map/all_to_all | solution.py:32
  128.3 0.1 reduce_sum.56
  128.5 9.7 %fusion = f32[8,80,4864]{2,1,0:T(8,128)} fusion(bf16[8,80,4864]{2,1,0:T(8,128)(2,1)} %param.8, bf16[512,4864,1]{1,0,2:T(8,128)(2,1)} %bitcast.30, f32[80,4864]{1,0:T(8,128)S(1)} %broadcast_subtract_fusion, f32[8,512]{1,0:T(8,128)S(1)} %broadcast_multiply_fusion, f32[80,512]{1,0:T(8,128)S(1)} %convert_bitcast_fusion), kind=kOutput, calls=%fused_computation.6 | convolution fusion | flops 3197665280 | bytes 25395200 | tf_op jit(solution)/shard_map/dot_general | solution.py:77
  138.2 46.7 %while.10 = (s32[]{:T(128)}, f32[8,8]{1,0:T(8,128)S(1)}, bf16[8,80,4864]{2,1,0:T(8,128)(2,1)}, f32[8,80,4864]{2,1,0:T(8,128)}, s32[]{:T(128)}, /*index=5*/s32[]{:T(128)}) while((s32[]{:T(128)}, f32[8,8]{1,0:T(8,128)S(1)}, bf16[8,80,4864]{2,1,0:T(8,128)(2,1)}, f32[8,80,4864]{2,1,0:T(8,128)}, s32[]{:T(128)}, /*index=5*/s32[]{:T(128)}) %tuple.23), condition=%wide.region_5.6_spmd, body=%wide.region_3.5_spmd.sunk | while | flops 9338874 | bytes 10895541 | solution.py:86
  138.2 1.5 dynamic-slice_bitcast_fusion.2
  139.7 4.3 %multiply_reduce_fusion.2 = f32[8]{0:T(128)S(1)} fusion(bf16[8,80,4864]{2,1,0:T(8,128)(2,1)} %get-tuple-element.74, f32[80,4864]{1,0:T(8,128)S(1)} %dynamic-slice_bitcast_fusion.2), kind=kLoop, calls=%fused_computation.2.clone.1 | loop fusion | flops 9338872 | bytes 7782432 | tf_op jit(solution)/shard_map/while/body/eval_jaxpr/reduce_sum | solution.py:84
  144.0 1.5 dynamic-slice_bitcast_fusion.2
  145.5 4.3 %multiply_reduce_fusion.2 = f32[8]{0:T(128)S(1)} fusion(bf16[8,80,4864]{2,1,0:T(8,128)(2,1)} %get-tuple-element.74, f32[80,4864]{1,0:T(8,128)S(1)} %dynamic-slice_bitcast_fusion.2), kind=kLoop, calls=%fused_computation.2.clone.1 | loop fusion | flops 9338872 | bytes 7782432 | tf_op jit(solution)/shard_map/while/body/eval_jaxpr/reduce_sum | solution.py:84
  149.9 1.5 dynamic-slice_bitcast_fusion.2
  151.4 4.3 %multiply_reduce_fusion.2 = f32[8]{0:T(128)S(1)} fusion(bf16[8,80,4864]{2,1,0:T(8,128)(2,1)} %get-tuple-element.74, f32[80,4864]{1,0:T(8,128)S(1)} %dynamic-slice_bitcast_fusion.2), kind=kLoop, calls=%fused_computation.2.clone.1 | loop fusion | flops 9338872 | bytes 7782432 | tf_op jit(solution)/shard_map/while/body/eval_jaxpr/reduce_sum | solution.py:84
  155.7 1.5 dynamic-slice_bitcast_fusion.2
  157.2 4.3 %multiply_reduce_fusion.2 = f32[8]{0:T(128)S(1)} fusion(bf16[8,80,4864]{2,1,0:T(8,128)(2,1)} %get-tuple-element.74, f32[80,4864]{1,0:T(8,128)S(1)} %dynamic-slice_bitcast_fusion.2), kind=kLoop, calls=%fused_computation.2.clone.1 | loop fusion | flops 9338872 | bytes 7782432 | tf_op jit(solution)/shard_map/while/body/eval_jaxpr/reduce_sum | solution.py:84
  161.5 1.5 dynamic-slice_bitcast_fusion.2
  163.0 4.3 %multiply_reduce_fusion.2 = f32[8]{0:T(128)S(1)} fusion(bf16[8,80,4864]{2,1,0:T(8,128)(2,1)} %get-tuple-element.74, f32[80,4864]{1,0:T(8,128)S(1)} %dynamic-slice_bitcast_fusion.2), kind=kLoop, calls=%fused_computation.2.clone.1 | loop fusion | flops 9338872 | bytes 7782432 | tf_op jit(solution)/shard_map/while/body/eval_jaxpr/reduce_sum | solution.py:84
  167.4 1.5 dynamic-slice_bitcast_fusion.2
  168.9 4.3 %multiply_reduce_fusion.2 = f32[8]{0:T(128)S(1)} fusion(bf16[8,80,4864]{2,1,0:T(8,128)(2,1)} %get-tuple-element.74, f32[80,4864]{1,0:T(8,128)S(1)} %dynamic-slice_bitcast_fusion.2), kind=kLoop, calls=%fused_computation.2.clone.1 | loop fusion | flops 9338872 | bytes 7782432 | tf_op jit(solution)/shard_map/while/body/eval_jaxpr/reduce_sum | solution.py:84
  173.2 1.5 dynamic-slice_bitcast_fusion.2
  174.7 4.3 %multiply_reduce_fusion.2 = f32[8]{0:T(128)S(1)} fusion(bf16[8,80,4864]{2,1,0:T(8,128)(2,1)} %get-tuple-element.74, f32[80,4864]{1,0:T(8,128)S(1)} %dynamic-slice_bitcast_fusion.2), kind=kLoop, calls=%fused_computation.2.clone.1 | loop fusion | flops 9338872 | bytes 7782432 | tf_op jit(solution)/shard_map/while/body/eval_jaxpr/reduce_sum | solution.py:84
  179.0 1.5 dynamic-slice_bitcast_fusion.2
  180.5 4.3 %multiply_reduce_fusion.2 = f32[8]{0:T(128)S(1)} fusion(bf16[8,80,4864]{2,1,0:T(8,128)(2,1)} %get-tuple-element.74, f32[80,4864]{1,0:T(8,128)S(1)} %dynamic-slice_bitcast_fusion.2), kind=kLoop, calls=%fused_computation.2.clone.1 | loop fusion | flops 9338872 | bytes 7782432 | tf_op jit(solution)/shard_map/while/body/eval_jaxpr/reduce_sum | solution.py:84
  184.9 0.1 copy.32
  184.9 9.6 %all_to_all.23 = f32[8,8,8]{2,1,0:T(8,128)S(1)} all-to-all(f32[8,8,8]{2,1,0:T(8,128)S(1)} %broadcast_in_dim.39), channel_id=1, replica_groups=mesh['occ_0'=8,'occ_1'=4,'occ_2'=2,'ao'=4] {'occ_2','ao'}, dimensions={0} | all-to-all | bytes 4096 | tf_op jit(solution)/shard_map/all_to_all | solution.py:32
  194.6 0.7 broadcast_in_dim.40
  195.3 3.9 %all-to-all-start.3 = ((f32[32,8,8]{2,1,0:T(8,128)}), f32[32,8,8]{2,1,0:T(8,128)S(1)}, u32[]{:S(2)}, u32[]{:S(2)}) async-start(f32[32,8,8]{2,1,0:T(8,128)} %broadcast_in_dim.40), calls=%async_computation.3 | async-start | bytes 262144 | tf_op jit(solution)/shard_map/all_to_all | solution.py:32
  199.2 0.1 reshape.101
  199.2 0.6 gather_fusion.1
  199.9 9.0 %all-to-all-done.3 = f32[32,8,8]{2,1,0:T(8,128)S(1)} async-done(((f32[32,8,8]{2,1,0:T(8,128)}), f32[32,8,8]{2,1,0:T(8,128)S(1)}, u32[]{:S(2)}, u32[]{:S(2)}) %all-to-all-start.3) | async-done | bytes 8224 | tf_op jit(solution)/shard_map/all_to_all | solution.py:32
  208.9 0.6 gather_fusion
  209.6 10.8 %fusion.2 = bf16[8,80,4864]{2,1,0:T(8,128)(2,1)} fusion(f32[8,80,4864]{2,1,0:T(8,128)} %get-tuple-element.81, bf16[8,80,4864]{2,1,0:T(8,128)(2,1)} %get-tuple-element.80, f32[8]{0:T(128)S(1)} %get-tuple-element.34), kind=kLoop, calls=%fused_computation.8 | loop fusion | flops 12451840 | bytes 24903712 | tf_op jit(solution)/shard_map/convert_element_type | solution.py:90
  220.3 0.7 rsqrt_multiply_fusion
  (35 shorter events, 0.4 us)
Async XLA Ops:
  7.2 66.4 %copy-start.1 = (bf16[512,80]{0,1:T(8,128)(2,1)S(1)}, bf16[512,80]{0,1:T(8,128)(2,1)}, u32[]{:S(2)}) copy-start(bf16[512,80]{0,1:T(8,128)(2,1)} %param.9) | copy-start | bytes 245764
  7.2 55.0 %all-gather.6.cloned.1.call-start = ((), (), s32[]{:S(2)}) async-start(), calls=%async_computation.4 | async-start | bytes 2801664 | tf_op jit(solution)/shard_map/all_gather | solution.py:19
  20.1 67.0 %all-gather.8.cloned.1.call-start = ((), (), s32[]{:S(2)}) async-start(), calls=%async_computation.5 | async-start | bytes 7471104 | tf_op jit(solution)/shard_map/all_gather | solution.py:19
  62.2 27.8 %slice-start = ((s8[6225920]{0:T(1024)(128)(4,1)}), s8[2031616]{0:T(1024)(128)(4,1)S(1)}, s32[]{:S(2)}) async-start(s8[6225920]{0:T(1024)(128)(4,1)} %bitcast.27), calls=%async_computation.6 | async-start | bytes 4063232
  87.1 3.7 %slice-start.1 = ((s8[6225920]{0:T(1024)(128)(4,1)}), s8[4194304]{0:T(1024)(128)(4,1)S(1)}, s32[]{:S(2)}) async-start(s8[6225920]{0:T(1024)(128)(4,1)} %bitcast.27), calls=%async_computation.7 | async-start | bytes 8388608
  90.0 4.2 %copy-start = (bf16[8,4,2,8,4864]{4,3,2,1,0:T(8,128)(2,1)}, bf16[8,4,2,8,4864]{4,3,2,1,0:T(8,128)(2,1)S(1)}, u32[]{:S(2)}) copy-start(bf16[8,4,2,8,4864]{4,3,2,1,0:T(8,128)(2,1)S(1)} %copy.27) | copy-start | bytes 14942212
  90.8 29.7 %copy-start.2 = (f32[4864]{0:T(1024)S(1)}, f32[4864]{0:T(1024)}, u32[]{:S(2)}) copy-start(f32[4864]{0:T(1024)} %param.12) | copy-start | bytes 58372
  90.8 29.7 %copy-start.4 = (f32[80]{0:T(128)S(1)}, f32[80]{0:T(128)}, u32[]{:S(2)}) copy-start(f32[80]{0:T(128)} %param.11) | copy-start | bytes 964
  90.8 37.7 %copy-start.3 = (f32[512]{0:T(512)S(1)}, f32[512]{0:T(512)}, u32[]{:S(2)}) copy-start(f32[512]{0:T(512)} %param.13) | copy-start | bytes 6148
  113.7 14.6 %all-to-all-start.1 = ((f32[8,1,4160]{2,1,0:T(1,128)}), f32[8,1,4160]{2,1,0:T(1,128)S(1)}, u32[]{:S(2)}, u32[]{:S(2)}) async-start(f32[8,1,4160]{2,1,0:T(1,128)} %broadcast_in_dim.22), calls=%async_computation.1 | async-start | bytes 270336 | tf_op jit(solution)/shard_map/all_to_all | solution.py:32
  195.3 13.6 %all-to-all-start.3 = ((f32[32,8,8]{2,1,0:T(8,128)}), f32[32,8,8]{2,1,0:T(8,128)S(1)}, u32[]{:S(2)}, u32[]{:S(2)}) async-start(f32[32,8,8]{2,1,0:T(8,128)} %broadcast_in_dim.40), calls=%async_computation.3 | async-start | bytes 262144 | tf_op jit(solution)/shard_map/all_to_all | solution.py:32
Sparse Core Ops, SparseCore 0:
  20.2 41.9 all-gather.5
  64.0 23.0 all-gather.7
where the time goes:
time: 229 us; the launch traced here: 228 us
  waiting for transfers between devices  72.3 us (32%)
  other arithmetic  46.5 us (20%)
  blocking collectives  40.7 us (18%)
  matrix products  24.3 us (11%)
  local copies, waits for them, and re-layouts  19.1 us (8%)
  between operations  14.2 us (6%)
  starting transfers between devices  10.7 us (5%)
    all_gather x2, waiting for transfers between devices, stacked_from(): tiles = lax.all_gather(tiles, axes[k])  55.6 us
    reduce_sum x8, other arithmetic, gram_column(): jnp.sum(amplitudes.astype(jnp.float32) * sigma_one[None], axis=(1, 2))  34.4 us
    all_to_all x2, blocking collectives, sent_to_all(): return lax.all_to_all(copies, axis, split_axis=0, concat_axis=0, tiled=True)  27.8 us
    all_to_all x2, waiting for transfers between devices, sent_to_all(): return lax.all_to_all(copies, axis, split_axis=0, concat_axis=0, tiled=True)  16.7 us
    all_gather x1, blocking collectives, stacked_from(): tiles = lax.all_gather(tiles, axes[k])  12.8 us
    mul x8, local copies, waits for them, and re-layouts, gram_column(): amplitudes.astype(jnp.float32) * sigma_one[None]  12.1 us
    dot_general x1, matrix products, shards(): jnp.dot(amps_rows, amps_rows.T, preferred_element_type=jnp.float32)  11.2 us
    convert_element_type x1, other arithmetic, shards(): (sigma_block - ritz_values[:, None, None] * amplitudes.astype(jnp.float32...  10.8 us
  transfers between devices with their start and end apart: 4, of which 4 were waited for; matrix products, arithmetic and copies ran while one was open for 5% of the time, Pallas kernels for 0%

commit v1 on v0

--- a/solution.py
+++ b/solution.py
@@ -56,6 +56,12 @@
     row_total = occ_coef.shape[0]
     flat_amps = amplitudes.reshape(trials * occ_dev, vir_dev)
     occ_trans = occ_coef.T.astype(jnp.float32)
+    energy_gaps = vir_energy[None, :] - occ_energy[:, None]
+    amps_rows = amplitudes.reshape(trials, occ_dev * vir_dev)
+    gap_rows = (energy_gaps[None] * amplitudes.astype(jnp.float32)).astype(jnp.bfloat16)
+    gap_rows = gap_rows.reshape(trials, occ_dev * vir_dev)
+    correlation_local = jnp.dot(amps_rows, amps_rows.T, preferred_element_type=jnp.float32)
+    gap_local = jnp.dot(amps_rows, gap_rows.T, preferred_element_type=jnp.float32)
     whole_rows = gather_axes(vir_coef, OCC, (1, 0, 2), 0)
     row_count = whole_rows.shape[0]
     half_done = lax.dot_general(
@@ -63,33 +69,23 @@
     )
     half_done = half_done.reshape(trials, occ_dev, row_count)
     partial_value = jnp.sum(half_done * occ_trans[None], axis=1)
-    amps_rows = amplitudes.reshape(trials, occ_dev * vir_dev)
-    correlation_local = jnp.dot(amps_rows, amps_rows.T, preferred_element_type=jnp.float32)
-    density, correlation = packed_total(
-        (partial_value, correlation_local), ("occ_0", ("occ_1", "occ_2", "ao"))
+    density, correlation, gap_gram = packed_total(
+        (partial_value, correlation_local, gap_local), ("occ_0", ("occ_1", "occ_2", "ao"))
     )
     potential = kernel[None, :] * density
+    gram = gap_gram + jnp.sum(density[:, None, :] * potential[None, :, :], axis=-1)
+    norms = jnp.diagonal(correlation) + 1e-06
+    ritz_values = jnp.diagonal(gram) / norms
     weighted = (
         (occ_trans[None] * potential[:, None, :])
         .astype(jnp.bfloat16)
         .reshape(trials * occ_dev, row_total)
     )
     coupling = jnp.dot(weighted, whole_rows, preferred_element_type=jnp.float32)
-    energy_gaps = vir_energy[None, :] - occ_energy[:, None]
-    sigma_block = energy_gaps[None] * amplitudes.astype(jnp.float32) + coupling.reshape(
-        trials, occ_dev, vir_dev
-    )
-
-    def gram_column(sigma_one):
-        return jnp.sum(amplitudes.astype(jnp.float32) * sigma_one[None], axis=(1, 2))
-
-    gram_local = lax.map(gram_column, sigma_block).T
-    gram = one_axis_at_a_time(gram_local, (("occ_0", "occ_1"), ("occ_2", "ao")))
-    norms = jnp.diagonal(correlation) + 1e-06
-    ritz_values = jnp.diagonal(gram) / norms
-    residual = (sigma_block - ritz_values[:, None, None] * amplitudes.astype(jnp.float32)).astype(
-        jnp.bfloat16
-    )
+    shifted = energy_gaps[None] - ritz_values[:, None, None]
+    residual = (
+        shifted * amplitudes.astype(jnp.float32) + coupling.reshape(trials, occ_dev, vir_dev)
+    ).astype(jnp.bfloat16)
     projected = gram / jnp.sqrt(norms[:, None] * norms[None, :])
     return (residual, projected)
 

time: 229 us -> 152 us (0.66)
  other arithmetic: 46.5 us -> 6.3 us
  waiting for transfers between devices: 72.3 us -> 51.4 us
  local copies, waits for them, and re-layouts: 19.1 us -> 5.61 us
  matrix products: 24.3 us -> 34.9 us
  starting transfers between devices: 10.7 us -> 3.45 us
  blocking collectives: 40.7 us -> 35.7 us
    reduce_sum x8 -> x1, other arithmetic: 34.4 us -> 0.09 us  [shards(): jnp.sum(density[:, None, :] * potential[None, :, :], axis=-1)]
    all_gather x2, waiting for transfers between devices: 55.6 us -> 43.3 us  [stacked_from(): tiles = lax.all_gather(tiles, axes[k])]
    mul x8 -> x1, local copies, waits for them, and re-layouts: 12.1 us -> 0.01 us  [shards(): density[:, None, :] * potential[None, :, :]]
    all_to_all x2 -> x1, waiting for transfers between devices: 16.7 us -> 8.06 us  [sent_to_all(): return lax.all_to_all(copies, axis, split_axis=0, concat_axis=0, tiled=True)]
    all_to_all x2 -> x1, starting transfers between devices: 10.6 us -> 3.37 us  [sent_to_all(): return lax.all_to_all(copies, axis, split_axis=0, concat_axis=0, tiled=True)]
    convert_element_type x1, other arithmetic: 10.8 us -> 4.02 us  [shards(): (energy_gaps[None] * amplitudes.astype(jnp.float32)).astype(jnp.bfloat16)]
    dot_general x0 -> x1, matrix products: none -> 6.52 us  [shards(): jnp.dot(amps_rows, gap_rows.T, preferred_element_type=jnp.float32)]
    all_to_all x2 -> x1, blocking collectives: 27.8 us -> 22.9 us  [sent_to_all(): return lax.all_to_all(copies, axis, split_axis=0, concat_axis=0, tiled=True)]
  transfers between devices with their start and end apart: 4 -> 3, of which waited for: 4 -> 3; matrix products, arithmetic and copies ran while one was open for 5% -> 16% of each run, Pallas kernels for 0% -> 0%
where the time goes in v1:
time: 152 us
  waiting for transfers between devices  51.4 us (34%)
  blocking collectives  35.7 us (23%)
  matrix products  34.9 us (23%)
  between operations  14.2 us (9%)
  other arithmetic  6.3 us (4%)
  local copies, waits for them, and re-layouts  5.61 us (4%)
  starting transfers between devices  3.45 us (2%)
    all_gather x2, waiting for transfers between devices, stacked_from(): tiles = lax.all_gather(tiles, axes[k])  43.3 us
    all_to_all x1, blocking collectives, sent_to_all(): return lax.all_to_all(copies, axis, split_axis=0, concat_axis=0, tiled=True)  22.9 us
    all_gather x1, blocking collectives, stacked_from(): tiles = lax.all_gather(tiles, axes[k])  12.8 us
    dot_general x1, matrix products, shards(): jnp.dot(amps_rows, amps_rows.T, preferred_element_type=jnp.float32)  11.8 us
    dot_general x1, matrix products, shards(): coupling = jnp.dot(weighted, whole_rows, preferred_element_type=jnp.float32)  8.63 us
    all_to_all x1, waiting for transfers between devices, sent_to_all(): return lax.all_to_all(copies, axis, split_axis=0, concat_axis=0, tiled=True)  8.06 us
    dot_general x1, matrix products, shards(): lax.dot_general(flat_amps, whole_rows, (((1,), (1,)), ((), ())), preferre...  7.98 us
    dot_general x1, matrix products, shards(): jnp.dot(amps_rows, gap_rows.T, preferred_element_type=jnp.float32)  6.52 us
  transfers between devices with their start and end apart: 3, of which 3 were waited for; matrix products, arithmetic and copies ran while one was open for 16% of the time, Pallas kernels for 0%

profile of v1, /device:TPU:1, one launch (start us, length us, event | category | flops | bytes accessed | tf_op | source)
XLA Modules:
  0.0 151.5 jit_solution(520159259528153314)
XLA Ops:
  7.2 0.0 all-gather.6.cloned.1.call-start
  7.2 12.8 %all-gather = bf16[32,4864]{1,0:T(8,128)(2,1)} all-gather(bf16[8,4864]{1,0:T(8,128)(2,1)} %param.8), channel_id=2, replica_groups=mesh['occ_0'=8,'occ_1'=4,'occ_2'=2,'ao'=4] {'occ_1'}, dimensions={0}, use_global_device_ids=true | all-gather | bytes 389120 | tf_op jit(solution)/shard_map/all_gather | solution.py:19
  20.0 0.0 all-gather.6.cloned.1.call-update
  20.0 0.0 all-gather.8.cloned.1.call-start
  20.1 42.1 %all-gather.6.cloned.1.call-done = bf16[32,8,4864]{2,1,0:T(8,128)(2,1)} async-done(((bf16[4,8,4864]{2,1,0:T(8,128)(2,1)}), bf16[32,8,4864]{2,1,0:T(8,128)(2,1)}) %all-gather.6.cloned.1.call-update) | async-done | bytes 2490384 | tf_op jit(solution)/shard_map/all_gather | solution.py:19
  62.2 0.0 all-gather.8.cloned.1.call-update
  62.2 0.0 slice-start
  62.2 1.1 broadcast_subtract_fusion
  63.3 0.0 slice-start.1
  63.3 4.0 %fusion = bf16[8,80,4864]{2,1,0:T(8,128)(2,1)S(1)} fusion(bf16[8,80,4864]{2,1,0:T(8,128)(2,1)} %param.6, f32[80,4864]{1,0:T(8,128)S(1)} %broadcast_subtract_fusion), kind=kLoop, calls=%fused_computation.4 | loop fusion | flops 9338880 | bytes 14008320 | tf_op jit(solution)/shard_map/convert_element_type | solution.py:61
  67.3 0.0 slice-done
  67.4 0.0 slice-done.1
  67.4 6.5 %fusion.12 = f32[8,8]{0,1:T(8,128)S(1)} fusion(bf16[8,80,4864]{2,1,0:T(8,128)(2,1)S(1)} %bitcast.24, bf16[8,80,4864]{2,1,0:T(8,128)(2,1)S(1)} %fusion), kind=kOutput, calls=%fused_computation.16 | convolution fusion | flops 49807360 | bytes 12452096 | tf_op jit(solution)/shard_map/dot_general | solution.py:64
  73.9 0.0 copy-start.1
  73.9 0.1 copy.36
  74.0 0.1 reshape.132
  74.0 11.8 %fusion.9 = f32[8,8]{1,0:T(8,128)S(1)} fusion(bf16[8,80,4864]{2,1,0:T(8,128)(2,1)} %param.6), kind=kOutput, calls=%fused_computation.15 | convolution fusion | flops 49807360 | bytes 6226176 | tf_op jit(solution)/shard_map/dot_general | solution.py:63
  85.8 0.1 reshape.131
  85.9 0.0 copy-done.1
  85.9 1.2 all-gather.8.cloned.1.call-done
  87.1 2.8 %copy.31 = bf16[8,4,2,8,4864]{4,3,2,1,0:T(8,128)(2,1)S(1)} copy(bf16[8,4,2,8,4864]{4,3,1,0,2:T(8,128)(2,1)} %bitcast.27) | data formatting | bytes 9961472 | tf_op jit(solution)/shard_map/transpose | solution.py:22
  89.8 0.0 copy-start
  89.9 0.0 copy-start.2
  89.9 8.0 %fusion.8 = f32[8,512]{1,0:T(8,128)S(1)} fusion(bf16[8,80,4864]{2,1,0:T(8,128)(2,1)} %param.6, bf16[512,4864,1]{1,0,2:T(8,128)(2,1)S(1)} %bitcast.25, f32[80,512]{1,0:T(8,128)S(1)} %convert_bitcast_fusion), kind=kOutput, calls=%fused_computation.14 | convolution fusion | flops 3188322304 | bytes 11386880 | tf_op jit(solution)/shard_map/dot_general | solution.py:67
  97.9 0.0 copy-done
  97.9 0.1 concatenate.8
  98.0 0.3 broadcast_in_dim.8
  98.2 22.9 %all_to_all.12 = f32[32,1,4224]{2,1,0:T(1,128)S(1)} all-to-all(f32[32,1,4224]{2,1,0:T(1,128)S(1)} %broadcast_in_dim.8), channel_id=1, replica_groups=mesh['occ_0'=8,'occ_1'=4,'occ_2'=2,'ao'=4] {'occ_1','occ_2','ao'}, dimensions={0} | all-to-all | bytes 1081344 | tf_op jit(solution)/shard_map/all_to_all | solution.py:32
  121.1 0.3 reduce_sum.37
  121.5 0.7 broadcast_in_dim.9
  122.2 3.4 %all-to-all-start.1 = ((f32[8,1,4224]{2,1,0:T(1,128)}), f32[8,1,4224]{2,1,0:T(1,128)S(1)}, u32[]{:S(2)}, u32[]{:S(2)}) async-start(f32[8,1,4224]{2,1,0:T(1,128)} %broadcast_in_dim.9), calls=%async_computation.1 | async-start | bytes 270336 | tf_op jit(solution)/shard_map/all_to_all | solution.py:32
  125.6 8.1 %all-to-all-done.1 = f32[8,1,4224]{2,1,0:T(1,128)S(1)} async-done(((f32[8,1,4224]{2,1,0:T(1,128)}), f32[8,1,4224]{2,1,0:T(1,128)S(1)}, u32[]{:S(2)}, u32[]{:S(2)}) %all-to-all-start.1) | async-done | bytes 135200 | tf_op jit(solution)/shard_map/all_to_all | solution.py:32
  133.6 0.1 reduce_sum.38
  133.8 0.1 fusion.20
  133.8 0.0 copy-done.2
  133.8 0.1 multiply_reduce_fusion
  133.9 0.1 reshape.134
  134.0 0.6 gather_fusion.1
  134.7 0.1 reshape.133
  134.7 0.7 rsqrt_multiply_fusion
  135.4 0.6 gather_fusion
  136.1 8.6 %fusion.2 = bf16[8,80,4864]{2,1,0:T(8,128)(2,1)} fusion(bf16[8,80,4864]{2,1,0:T(8,128)(2,1)} %param.6, bf16[512,4864,1]{1,0,2:T(8,128)(2,1)} %bitcast.26, f32[8]{0:T(128)S(1)} %fusion.19, f32[80,4864]{1,0:T(8,128)S(1)} %broadcast_subtract_fusion, f32[8,512]{1,0:T(8,128)S(1)} %broadcast_multiply_fusion, f32[80,512]{1,0:T(8,128)S(1)} %convert_bitcast_fusion), kind=kOutput, calls=%fused_computation.6 | convolution fusion | flops 3203891200 | bytes 19169312 | tf_op jit(solution)/shard_map/dot_general | solution.py:84
  (9 shorter events, 0.1 us)
Async XLA Ops:
  7.2 55.0 %all-gather.6.cloned.1.call-start = ((), (), s32[]{:S(2)}) async-start(), calls=%async_computation.2 | async-start | bytes 2801664 | tf_op jit(solution)/shard_map/all_gather | solution.py:19
  20.0 67.0 %all-gather.8.cloned.1.call-start = ((), (), s32[]{:S(2)}) async-start(), calls=%async_computation.3 | async-start | bytes 7471104 | tf_op jit(solution)/shard_map/all_gather | solution.py:19
  62.2 5.1 %slice-start = ((s8[6225920]{0:T(1024)(128)(4,1)}), s8[4194304]{0:T(1024)(128)(4,1)S(1)}, s32[]{:S(2)}) async-start(s8[6225920]{0:T(1024)(128)(4,1)} %bitcast.23), calls=%async_computation.4 | async-start | bytes 8388608
  63.3 4.0 %slice-start.1 = ((s8[6225920]{0:T(1024)(128)(4,1)}), s8[2031616]{0:T(1024)(128)(4,1)S(1)}, s32[]{:S(2)}) async-start(s8[6225920]{0:T(1024)(128)(4,1)} %bitcast.23), calls=%async_computation.5 | async-start | bytes 4063232
  73.9 12.0 %copy-start.1 = (bf16[512,80]{0,1:T(8,128)(2,1)S(1)}, bf16[512,80]{0,1:T(8,128)(2,1)}, u32[]{:S(2)}) copy-start(bf16[512,80]{0,1:T(8,128)(2,1)} %param.7) | copy-start | bytes 245764
  89.8 8.0 %copy-start = (bf16[8,4,2,8,4864]{4,3,2,1,0:T(8,128)(2,1)}, bf16[8,4,2,8,4864]{4,3,2,1,0:T(8,128)(2,1)S(1)}, u32[]{:S(2)}) copy-start(bf16[8,4,2,8,4864]{4,3,2,1,0:T(8,128)(2,1)S(1)} %copy.31) | copy-start | bytes 14942212
  89.9 44.0 %copy-start.2 = (f32[512]{0:T(512)S(1)}, f32[512]{0:T(512)}, u32[]{:S(2)}) copy-start(f32[512]{0:T(512)} %param.11) | copy-start | bytes 6148
  122.2 11.5 %all-to-all-start.1 = ((f32[8,1,4224]{2,1,0:T(1,128)}), f32[8,1,4224]{2,1,0:T(1,128)S(1)}, u32[]{:S(2)}, u32[]{:S(2)}) async-start(f32[8,1,4224]{2,1,0:T(1,128)} %broadcast_in_dim.9), calls=%async_computation.1 | async-start | bytes 270336 | tf_op jit(solution)/shard_map/all_to_all | solution.py:32
Sparse Core Ops, SparseCore 0:
  20.2 42.0 all-gather.5
  64.0 23.0 all-gather.7

commit v2 on v1

v2 whole, which is shorter than its diff:
```python
import functools

import jax
import jax.numpy as jnp
from jax import lax
from jax.experimental import pallas as pl
from jax.experimental.pallas import tpu as pltpu
from jax.sharding import PartitionSpec as P

F32 = jnp.float32
BF16 = jnp.bfloat16
MESH = pl.DeviceIdType.MESH
NZ, NY, NC, NX = 8, 4, 2, 4
K, I, M, A = 8, 80, 512, 4864
FIRST = (0, 2048)
SECOND = (2048, 4864)
PARTS = (FIRST, SECOND)
EXTRA = 128
WIDE = M + EXTRA
SLICES = ((0, 1024), (1024, 2048), (2048, 3072), (3072, 4096), (4096, 4864))
AMP_CUTS = ((0, 1280), (1280, 2560), (2560, 3840), (3840, 4864))


def signed(d, n):
    return d if d <= n // 2 else d - n


def columns_of(part, half):
    low, high = PARTS[part]
    middle = (low + high) // 2
    return {None: (low, high), 0: (low, middle), 1: (middle, high)}[half]


def onward(part, half, dy, dz):
    sy, sz = signed(dy, NY), signed(dz, NZ)
    out = []
    if part == 0:
        if sz == 0:
            if sy == 0:
                out += [(None, 1, 0), (None, -1, 0)]
            elif sy == -1:
                out.append((0, 1, 0))
            elif sy == 1:
                out.append((1, -1, 0))
            out += [(None, 0, 1), (None, 0, -1)]
        elif sz in (-1, -2):
            out.append((None, 0, 1))
        elif sz == -3:
            out.append((0, 0, 1))
        elif sz in (1, 2):
            out.append((None, 0, -1))
        elif sz == 3:
            out.append((1, 0, -1))
    else:
        if sy == 0:
            if sz in (0, -1, -2):
                out.append((None, 0, 1))
            if sz in (0, 1, 2):
                out.append((None, 0, -1))
            if sz == -3:
                out.append((0, 0, 1))
            if sz == 3:
                out.append((1, 0, -1))
            out += [(None, 1, 0), (None, -1, 0)]
        elif sy == -1:
            out.append((0, 1, 0))
        elif sy == 1:
            out.append((1, -1, 0))
    return out


def halves_of(part, dy, dz):
    sy, sz = signed(dy, NY), signed(dz, NZ)
    if part == 0:
        split = sz == 4 or (sz == 0 and sy == 2)
    else:
        split = sy == 2 or (sy == 0 and sz == 4)
    return (0, 1) if split else (None,)


LEVELS = [
    [
        (part, dy, dz)
        for dz in (0, 7, 1, 6, 2, 5, 3, 4)
        for dy in (0, 3, 1, 2)
        for part in (1, 0)
        if abs(signed(dy, NY)) + abs(signed(dz, NZ)) == level
    ]
    for level in range(7)
]


def gather_kernel(
    vir_ref,
    amps_ref,
    occ_ref,
    occ_e_ref,
    vir_e_ref,
    rows_ref,
    amps_out,
    total_ref,
    half_acc,
    corr_acc,
    gap_acc,
    za,
    ya,
    xa,
    link_send,
    link_recv,
    pair_send,
    pair_recv,
    local_sem,
    amp_sem,
    z_send,
    z_recv,
    y_send,
    y_recv,
    x_send,
    x_recv,
):
    me = lax.axis_index("occ")
    x = lax.axis_index("ao")
    z, y, c = me // (NY * NC), (me // NC) % NY, me % NC

    def at(zz, yy, cc):
        return lax.rem(zz + 2 * NZ, NZ) * (NY * NC) + lax.rem(yy + 2 * NY, NY) * NC + cc

    barrier = pltpu.get_barrier_semaphore()
    near = [(at(z, y + 1, c), x), (at(z, y - 1, c), x), (at(z + 1, y, c), x), (at(z - 1, y, c), x)]
    near.append((at(z, y, 1 - c), x))
    near += [(me, lax.rem(x + d, NX)) for d in (1, 2, 3)]
    for device in near:
        pl.semaphore_signal(barrier, inc=1, device_id=device, device_id_type=MESH)

    def rows_at(dy, dz, cc):
        start = pl.multiple_of(at(z + signed(dz, NZ), y + signed(dy, NY), cc) * 8, 8)
        return pl.ds(start, 8)

    own = pltpu.make_async_copy(vir_ref, rows_ref.at[rows_at(0, 0, c), :], local_sem)
    own.start()
    amp_copies = []
    for n, (low, high) in enumerate(AMP_CUTS):
        amp_copies.append(
            pltpu.make_async_copy(
                amps_ref.at[:, pl.ds(low, high - low)],
                amps_out.at[:, pl.ds(low, high - low)],
                amp_sem.at[n],
            )
        )
    for copy in amp_copies:
        copy.start()
    own.wait()
    pl.semaphore_wait(barrier, len(near))

    sent = []

    def piece(part, half, dy, dz, cc):
        low, high = columns_of(part, half)
        return rows_ref.at[rows_at(dy, dz, cc), pl.ds(low, high - low)]

    def recv_index(part, half, dy, dz):
        return ((part * 2 + (half or 0)) * NY + dy) * NZ + dz

    def link_copy(part, half, dy, dz, step_y, step_z):
        block = piece(part, half, dy, dz, c)
        return pltpu.make_async_remote_copy(
            src_ref=block,
            dst_ref=block,
            send_sem=link_send.at[len(sent)],
            recv_sem=link_recv.at[
                recv_index(part, half, (dy - step_y) % NY, (dz - step_z) % NZ)
            ],
            device_id=(at(z + step_z, y + step_y, c), x),
            device_id_type=MESH,
        )

    def arrival(part, half, dy, dz):
        block = piece(part, half, dy, dz, c)
        return pltpu.make_async_copy(block, block, link_recv.at[recv_index(part, half, dy, dz)])

    def pair_copy(part, dy, dz):
        block = piece(part, None, dy, dz, c)
        index = (part * NY + dy) * NZ + dz
        return pltpu.make_async_remote_copy(
            src_ref=block,
            dst_ref=block,
            send_sem=pair_send.at[index],
            recv_sem=pair_recv.at[index],
            device_id=(at(z, y, 1 - c), x),
            device_id_type=MESH,
        )

    pair_copies = []

    def pass_on(part, dy, dz):
        for half, step_y, step_z in onward(part, None, dy, dz):
            copy = link_copy(part, half, dy, dz, step_y, step_z)
            copy.start()
            sent.append(copy)
        copy = pair_copy(part, dy, dz)
        copy.start()
        pair_copies.append(copy)

    def receive(part, dy, dz):
        for half in halves_of(part, dy, dz):
            arrival(part, half, dy, dz).wait()
        pass_on(part, dy, dz)

    def pair_arrival(part, dy, dz):
        block = piece(part, None, dy, dz, 1 - c)
        pltpu.make_async_copy(
            block, block, pair_recv.at[(part * NY + dy) * NZ + dz]
        ).wait()

    square = (lax.broadcasted_iota(jnp.int32, (I, I), 0), lax.broadcasted_iota(jnp.int32, (I, I), 1))
    occ_e = jnp.sum(
        jnp.where(square[0] == square[1], jnp.broadcast_to(occ_e_ref[...], (I, I)), 0.0),
        axis=1,
        keepdims=True,
    )

    def trial_sums(block):
        corr = jnp.zeros((128, 128), F32)
        gaps = jnp.zeros((128, 128), F32)
        for low, high in SLICES:
            rows = [amps_out[k * I + block * 16 : k * I + block * 16 + 16, low:high] for k in range(K)]
            chunk = jnp.concatenate(rows, axis=0)
            scaled = (chunk.astype(F32) * vir_e_ref[:, low:high]).astype(BF16)
            dims = (((1,), (1,)), ((), ()))
            corr += lax.dot_general(chunk, chunk, dims, preferred_element_type=F32)
            gaps += lax.dot_general(chunk, scaled, dims, preferred_element_type=F32)
        levels = jnp.concatenate([occ_e[block * 16 : block * 16 + 16]] * K, axis=0)
        gaps -= levels * corr
        if block == 0:
            corr_acc[...] = corr
            gap_acc[...] = gaps
        else:
            corr_acc[...] += corr
            gap_acc[...] += gaps

    def trial_totals():
        r = lax.broadcasted_iota(jnp.int32, (128, 128), 0)
        q = lax.broadcasted_iota(jnp.int32, (128, 128), 1)
        same = (r % 16) == (q % 16)
        pick = lax.broadcasted_iota(jnp.int32, (128, EXTRA), 0) // 16
        lane = lax.broadcasted_iota(jnp.int32, (128, EXTRA), 1)
        out = jnp.zeros((K, EXTRA), F32)
        for n, acc in enumerate((corr_acc, gap_acc)):
            kept = jnp.where(same, acc[...], 0.0)
            summed = jnp.sum(kept.reshape(K, 16, 128), axis=1)
            chosen = (pick + n * K == lane).astype(F32)
            out += jnp.dot(
                summed, chosen, precision=lax.Precision.HIGHEST, preferred_element_type=F32
            )
        return out

    def half_done(group, low, high):
        rows = []
        for n in range(4):
            start = lax.rem(z + NZ - 2 + group * 4 + n, NZ) * 64
            rows.append(rows_ref[pl.ds(pl.multiple_of(start, 64), 64), low:high])
        vir = jnp.concatenate(rows, axis=0)
        part = lax.dot_general(
            amps_out[:, low:high], vir, (((1,), (1,)), ((), ())), preferred_element_type=F32
        )
        if low == 0:
            half_acc[...] = part
        else:
            half_acc[...] += part

    turn = lax.rem(z + NZ - 2, NZ) * 64
    occ_rel = pltpu.roll(occ_ref[...].astype(F32), lax.rem(M - turn, M), 1)

    def partial_density(group):
        occ = occ_rel[:, group * 256 : group * 256 + 256]
        rows = []
        for k in range(K):
            rows.append(jnp.sum(half_acc[k * I : k * I + I, :] * occ, axis=0, keepdims=True))
        return jnp.concatenate(rows, axis=0)

    for part, dy, dz in LEVELS[0]:
        pass_on(part, dy, dz)
    for copy in amp_copies:
        copy.wait()
    trial_sums(0)
    trial_sums(1)
    for step in LEVELS[1]:
        receive(*step)
    trial_sums(2)
    for step in LEVELS[2]:
        receive(*step)
    trial_sums(3)
    for step in LEVELS[3]:
        receive(*step)
    trial_sums(4)
    extra = trial_totals()
    for step in LEVELS[4]:
        receive(*step)
    early = [(p, dy, dz) for p in (0, 1) for dy in range(NY) for dz in (6, 7, 0, 1)]
    late = [(p, dy, dz) for p in (0, 1) for dy in range(NY) for dz in (2, 3, 4, 5)]
    for step in early:
        pair_arrival(*step)
    half_done(0, *SLICES[0])
    half_done(0, *SLICES[1])
    for step in LEVELS[5]:
        receive(*step)
    for cut in SLICES[2:]:
        half_done(0, *cut)
    first = partial_density(0)
    for step in LEVELS[6]:
        receive(*step)
    for step in late:
        pair_arrival(*step)
    for cut in SLICES:
        half_done(1, *cut)
    second = partial_density(1)
    density = pltpu.roll(jnp.concatenate([first, second], axis=1), turn, 1)

    def all_sum(slots, mine, count, send, recv, device_of):
        copies = []
        for d in range(1, count):
            copies.append(
                pltpu.make_async_remote_copy(
                    src_ref=slots.at[mine],
                    dst_ref=slots.at[mine],
                    send_sem=send.at[d],
                    recv_sem=recv.at[(count - d) % count],
                    device_id=device_of(d),
                    device_id_type=MESH,
                )
            )
        for copy in copies:
            copy.start()
        for d in range(1, count):
            other = slots.at[lax.rem(mine + d, count)]
            pltpu.make_async_copy(other, other, recv.at[d]).wait()
        out = slots[0]
        for n in range(1, count):
            out = out + slots[n]
        return out, copies

    za[z, :, :M] = density
    za[z, :, M:] = extra
    total, z_copies = all_sum(
        za, z, NZ, z_send, z_recv, lambda d: (at(z + d, y, c), x)
    )
    place = y * NC + c
    ya[place] = total
    total, y_copies = all_sum(
        ya,
        place,
        NY * NC,
        y_send,
        y_recv,
        lambda d: (z * (NY * NC) + lax.rem(place + d, NY * NC), x),
    )
    xa[x] = total
    total, x_copies = all_sum(
        xa, x, NX, x_send, x_recv, lambda d: (me, lax.rem(x + d, NX))
    )
    total_ref[...] = total
    for copy in sent + pair_copies + z_copies + y_copies + x_copies:
        copy.wait_send()


SENDS = sum(
    len(onward(part, None, dy, dz)) for level in LEVELS for part, dy, dz in level
)
BLOCKS = [(n * 256, n * 256 + 256) for n in range(A // 256)]


def residual_kernel(
    rows_ref,
    amps_ref,
    total_ref,
    occ_ref,
    occ_e_ref,
    vir_e_ref,
    kernel_ref,
    out_ref,
    projected_ref,
    weighted,
    staged,
    out_sem,
):
    density = total_ref[:, :M]
    correlation = total_ref[:, M : M + K]
    gap_gram = total_ref[:, M + K : M + 2 * K]
    potential = kernel_ref[...] * density
    occ = occ_ref[...].astype(F32)
    for k in range(K):
        weighted[k * I : k * I + I, :] = (occ * potential[k : k + 1, :]).astype(BF16)
    lane = lax.broadcasted_iota(jnp.int32, (K, K), 1)
    row = lax.broadcasted_iota(jnp.int32, (K, K), 0)
    gram = gap_gram
    for m in range(K):
        column = jnp.sum(density * potential[m : m + 1, :], axis=1, keepdims=True)
        gram = gram + jnp.where(lane == m, column, 0.0)
    diagonal = lane == row
    kept = jnp.where(diagonal, correlation, 0.0)
    norm_col = jnp.sum(kept, axis=1, keepdims=True) + 1e-6
    norm_row = jnp.sum(kept, axis=0, keepdims=True) + 1e-6
    projected_ref[...] = gram / jnp.sqrt(norm_col * norm_row)
    ritz = jnp.sum(jnp.where(diagonal, gram, 0.0), axis=1, keepdims=True) / norm_col
    square = (lax.broadcasted_iota(jnp.int32, (I, I), 0), lax.broadcasted_iota(jnp.int32, (I, I), 1))
    occ_e = jnp.sum(
        jnp.where(square[0] == square[1], jnp.broadcast_to(occ_e_ref[...], (I, I)), 0.0),
        axis=1,
        keepdims=True,
    )
    copies = []
    for n, (low, high) in enumerate(BLOCKS):
        coupling = jnp.dot(weighted[...], rows_ref[:, low:high], preferred_element_type=F32)
        for k in range(K):
            shift = occ_e + ritz[k : k + 1, :]
            gaps = vir_e_ref[:, low:high] - shift
            rows = slice(k * I, k * I + I)
            staged[rows, low:high] = (
                gaps * amps_ref[rows, low:high].astype(F32) + coupling[rows]
            ).astype(BF16)
        copy = pltpu.make_async_copy(
            staged.at[:, pl.ds(low, high - low)], out_ref.at[:, pl.ds(low, high - low)], out_sem.at[n]
        )
        copy.start()
        copies.append(copy)
    for copy in copies:
        copy.wait()


def shards(amplitudes, occ_coef, vir_coef, occ_energy, vir_energy, kernel):
    amps = amplitudes.reshape(K * I, A)
    occ = occ_coef.T
    occ_e = occ_energy.reshape(1, I)
    vir_e = vir_energy.reshape(1, A)
    vmem = pl.BlockSpec(memory_space=pltpu.VMEM)
    hbm = pl.BlockSpec(memory_space=pl.ANY)
    dma = pltpu.SemaphoreType.DMA
    rows, amps_in, total = pl.pallas_call(
        gather_kernel,
        out_shape=(
            pltpu.VMEM((M, A), BF16),
            pltpu.VMEM((K * I, A), BF16),
            pltpu.VMEM((K, WIDE), F32),
        ),
        in_specs=[hbm, hbm, vmem, vmem, vmem],
        out_specs=(vmem, vmem, vmem),
        scratch_shapes=[
            pltpu.VMEM((K * I, 256), F32),
            pltpu.VMEM((128, 128), F32),
            pltpu.VMEM((128, 128), F32),
            pltpu.VMEM((NZ, K, WIDE), F32),
            pltpu.VMEM((NY * NC, K, WIDE), F32),
            pltpu.VMEM((NX, K, WIDE), F32),
            dma((SENDS,)),
            dma((2 * 2 * NY * NZ,)),
            dma((2 * NY * NZ,)),
            dma((2 * NY * NZ,)),
            dma,
            dma((len(AMP_CUTS),)),
            dma((NZ,)),
            dma((NZ,)),
            dma((NY * NC,)),
            dma((NY * NC,)),
            dma((NX,)),
            dma((NX,)),
        ],
        compiler_params=pltpu.CompilerParams(
            collective_id=0, has_side_effects=True, vmem_limit_bytes=20 * 2**20
        ),
        name="gather_and_reduce",
    )(vir_coef, amps, occ, occ_e, vir_e)
    residual, projected = pl.pallas_call(
        residual_kernel,
        out_shape=(
            jax.ShapeDtypeStruct((K * I, A), BF16),
            jax.ShapeDtypeStruct((K, K), F32),
        ),
        in_specs=[vmem] * 7,
        out_specs=(hbm, vmem),
        scratch_shapes=[
            pltpu.VMEM((K * I, M), BF16),
            pltpu.VMEM((K * I, A), BF16),
            dma((len(BLOCKS),)),
        ],
        compiler_params=pltpu.CompilerParams(vmem_limit_bytes=20 * 2**20),
        name="residual",
    )(rows, amps_in, total, occ, occ_e, vir_e, kernel.reshape(1, M))
    return residual.reshape(K, I, A), projected


def solution(mesh):
    in_specs = (P(None, "occ", "ao"), P(None, "occ"), P("occ", "ao"), P("occ"), P("ao"), P())
    out_specs = (P(None, "occ", "ao"), P())
    return jax.shard_map(
        shards, mesh=mesh, in_specs=in_specs, out_specs=out_specs, check_vma=False
    )
```

time: 152 us -> 69.9 us (0.46)
  Pallas kernels: 0 us -> 63.1 us
  waiting for transfers between devices: 51.4 us -> 0 us
  blocking collectives: 35.7 us -> 0 us
  matrix products: 34.9 us -> 0 us
  between operations: 14.2 us -> 0.67 us
  other arithmetic: 6.3 us -> 0 us
  starting transfers between devices: 3.45 us -> 0 us
    pallas_call x0 -> x2, Pallas kernels: none -> 63.1 us  [the longest x1 57.5 us: shards(): pl.pallas_call(gather_kernel, out_shape=(pltpu.VMEM((M, A), BF16), pltpu....]
    all_gather x2 -> x0, waiting for transfers between devices: 43.3 us -> none  [stacked_from(): tiles = lax.all_gather(tiles, axes[k])]
    dot_general x4 -> x0, matrix products: 34.9 us -> none  [the longest x1 11.8 us: shards(): jnp.dot(amps_rows, amps_rows.T, preferred_element_type=jnp.float32)]
    all_to_all x1 -> x0, blocking collectives: 22.9 us -> none  [sent_to_all(): return lax.all_to_all(copies, axis, split_axis=0, concat_axis=0, tiled=True)]
    all_gather x1 -> x0, blocking collectives: 12.8 us -> none  [stacked_from(): tiles = lax.all_gather(tiles, axes[k])]
    all_to_all x1 -> x0, waiting for transfers between devices: 8.06 us -> none  [sent_to_all(): return lax.all_to_all(copies, axis, split_axis=0, concat_axis=0, tiled=True)]
    unnamed x11 -> x10, local copies, waits for them, and re-layouts: 0.04 us -> 5.19 us
    convert_element_type x2 -> x0, other arithmetic: 4.03 us -> none  [the longest x1 4.02 us: shards(): (energy_gaps[None] * amplitudes.astype(jnp.float32)).astype(jnp.bfloat16)]
  transfers between devices with their start and end apart: 3 -> 0, of which waited for: 3 -> 0; matrix products, arithmetic and copies ran while one was open for 16% -> 0% of each run, Pallas kernels for 0% -> 0%
where the time goes in v2:
time: 69.9 us; the launch traced here: 69.7 us
  Pallas kernels  63.1 us (90%)
  local copies, waits for them, and re-layouts  5.94 us (8%)
    pallas_call x1, Pallas kernels, shards(): pl.pallas_call(gather_kernel, out_shape=(pltpu.VMEM((M, A), BF16), pltpu....  57.5 us
    pallas_call x1, Pallas kernels, shards(): pl.pallas_call(residual_kernel, out_shape=(jax.ShapeDtypeStruct((K * I, A...  5.54 us
    unnamed x10, local copies, waits for them, and re-layouts  5.19 us

profile of v2, /device:TPU:1, one launch (start us, length us, event | category | flops | bytes accessed | tf_op | source)
XLA Modules:
  0.0 69.7 jit_solution(1273891637350823219)
XLA Ops:
  0.6 0.0 copy-start.3
  0.6 0.7 %reshape.21.vir_e_ref = f32[1,4864]{1,0:T(1,128)S(1)} reshape(f32[4864]{0:T(1024)} %param.10) | data formatting | bytes 38912 | tf_op jit(solution)/shard_map/reshape | solution.py:434
  1.4 0.0 copy-start
  1.4 2.8 %copy-done = bf16[8,80,4864]{2,1,0:T(8,128)(2,1)S(1)} copy-done((bf16[8,80,4864]{2,1,0:T(8,128)(2,1)S(1)}, bf16[8,80,4864]{2,1,0:T(8,128)(2,1)}, u32[]{:S(2)}) %copy-start) | copy-done | bytes 6225944
  4.2 0.0 copy-start.1
  4.2 0.9 %copy-done.1 = bf16[512,80]{0,1:T(8,128)(2,1)S(1)} copy-done((bf16[512,80]{0,1:T(8,128)(2,1)S(1)}, bf16[512,80]{0,1:T(8,128)(2,1)}, u32[]{:S(2)}) %copy-start.1) | copy-done | bytes 81944
  5.0 0.0 copy-start.2
  5.0 0.9 %copy-done.2 = bf16[8,4864]{1,0:T(8,128)(2,1)S(1)} copy-done((bf16[8,4864]{1,0:T(8,128)(2,1)S(1)}, bf16[8,4864]{1,0:T(8,128)(2,1)}, u32[]{:S(2)}) %copy-start.2) | copy-done | bytes 77848
  5.9 0.0 copy-start.4
  5.9 0.7 copy-done.4
  6.6 57.5 %gather_and_reduce.1 = (bf16[512,4864]{1,0:T(8,128)(2,1)S(1)}, bf16[640,4864]{1,0:T(8,128)(2,1)S(1)}, f32[8,640]{1,0:T(8,128)S(1)}) custom-call(bf16[8,4864]{1,0:T(8,128)(2,1)S(1)} %copy-done.2, bf16[640,4864]{1,0:T(8,128)(2,1)S(1)} %bitcast.5, bf16[80,512]{1,0:T(8,128)(2,1)S(1)} %bitcast.6, f32[1,80]{1,0:T(1,128)S(1)} %bitcast.9, ...), custom_call_target="tpu_custom_call" | custom-call | tf_op jit(solution)/shard_map/gather_and_reduce/pallas_call | solution.py:438
  64.1 0.0 copy-done.3
  64.1 5.5 %residual.1 = (bf16[640,4864]{1,0:T(8,128)(2,1)}, f32[8,8]{1,0:T(8,128)}) custom-call(bf16[512,4864]{1,0:T(8,128)(2,1)S(1)} %get-tuple-element.7.rows_ref, bf16[640,4864]{1,0:T(8,128)(2,1)S(1)} %get-tuple-element.8.amps_ref, f32[8,640]{1,0:T(8,128)S(1)} %get-tuple-element.9.total_ref, bf16[80,512]{1,0:T(8,128)(2,1)S(1)} %bitcast.7, f32[1,80]{1,0:T(1,128)S(1)} %bitcast.10, ...), custom_call_target="tpu_custom_call" | custom-call | tf_op jit(solution)/shard_map/residual/pallas_call | solution.py:472
Async XLA Ops:
  0.6 63.5 %copy-start.3 = (f32[512]{0:T(512)S(1)}, f32[512]{0:T(512)}, u32[]{:S(2)}) copy-start(f32[512]{0:T(512)} %param.11) | copy-start | bytes 6148
  1.4 2.8 %copy-start = (bf16[8,80,4864]{2,1,0:T(8,128)(2,1)S(1)}, bf16[8,80,4864]{2,1,0:T(8,128)(2,1)}, u32[]{:S(2)}) copy-start(bf16[8,80,4864]{2,1,0:T(8,128)(2,1)} %param.6) | copy-start | bytes 18677764
  4.2 0.9 %copy-start.1 = (bf16[512,80]{0,1:T(8,128)(2,1)S(1)}, bf16[512,80]{0,1:T(8,128)(2,1)}, u32[]{:S(2)}) copy-start(bf16[512,80]{0,1:T(8,128)(2,1)} %param.7) | copy-start | bytes 245764
  5.0 0.9 %copy-start.2 = (bf16[8,4864]{1,0:T(8,128)(2,1)S(1)}, bf16[8,4864]{1,0:T(8,128)(2,1)}, u32[]{:S(2)}) copy-start(bf16[8,4864]{1,0:T(8,128)(2,1)} %vir_ref.1) | copy-start | bytes 233476
  5.9 0.7 copy-start.4
